TPU v7x, 32 devices: a whole 2x2x4 slice. The times are simulated.
32 devices in a mesh: loader: 8 (over z, x), split: 4 (over y, core).
Axes of the slice: x: 2, y: 2, z: 4, core: 2. Of those that a mesh axis runs over, the one named last changes fastest.
Arguments:
- embeddings: bfloat16 [16384, 768], P(('loader', 'split')), may hold values from -6 to 6
- cluster_ids: int32 [16384, 1], P(('loader', 'split')), may hold values from 0 to 255; in each aligned block of 512 rows (0 to 511, 512 to 1023, ...) at most 4 rows name the same one
- ranks: int32 [16384], P(('loader', 'split')), may hold values from 0 to 16383, each once
Outputs:
- nearest: float32 [16384], P(('loader', 'split'))
Inputs may be any that keep to these rules, and one draw needn't show every extreme that they name: `cluster_ids`: among the 512 rows of one device no cluster appears more than 4 times. All ranks differ.
All inputs are finite; a program needn't handle non-finite values.
Results may differ from a plain program's by a relative error of at most 0.0014.
Values may be sent and summed in bfloat16 or wider, within the bound.
A program may use at most 64 MiB of HBM per device.

v0:
```python
import functools

import jax
import jax.numpy as jnp
from jax import lax
from jax.experimental import pallas as pl
from jax.experimental.pallas import tpu as pltpu
from jax.sharding import PartitionSpec as P

CLUSTERS = 256
CAP = 4
LANES = 128
TILE = 16

epsilon = 1e-06
EXACT = lax.Precision.HIGHEST
NN = (((1,), (0,)), ((), ()))
NT = (((1,), (1,)), ((), ()))
TN = (((0,), (0,)), ((), ()))
QUARTERS = (2, 1, 3, 0)


def dot(a, b, dims, precision=None):
    return lax.dot_general(a, b, dims, precision=precision, preferred_element_type=jnp.float32)


def iota(shape, axis):
    return lax.broadcasted_iota(jnp.int32, shape, axis)


def column(row):
    return jnp.transpose(jnp.broadcast_to(row, (LANES, row.shape[1])))[:, :1]


def kernel(n, splits, chunks, big, emb_hbm, cid_hbm, rank_hbm, out_ref, over_ref, *scratch):
    pieces = len(chunks)
    rows_out, rows_in = scratch[:pieces], scratch[pieces : 2 * pieces]
    (
        keys_out, keys_in, best_out, best_in,
        rows_out_sem, rows_in_sem, keys_out_sem, keys_in_sem, best_out_sem, best_in_sem, own_sem,
        emb_ref, cid_ref, rank_ref, load_sem,
    ) = scratch[2 * pieces :]
    me = lax.axis_index("loader") * splits + lax.axis_index("split")
    count, width = emb_hbm.shape
    quarter = n // 4
    mine, inner = me // quarter, me % quarter
    sign = 1 - 2 * (mine // 2)
    starts = [sum(chunks[:i]) for i in range(pieces)]

    def where_is(index):
        return {"loader": index // splits, "split": index % splits}

    def quarter_of(turn):
        return (mine + sign * QUARTERS[turn] + 4) % 4

    def each(act, turns=range(4)):
        for turn in turns:
            base = quarter_of(turn) * quarter
            first = 1 if QUARTERS[turn] == 0 else 0

            def step(i, carry):
                act(base + (inner + i) % quarter)
                return carry

            lax.fori_loop(first, quarter, step, 0)

    def remote(source, target, send, receive, peer):
        return pltpu.make_async_remote_copy(
            src_ref=source, dst_ref=target, send_sem=send, recv_sem=receive,
            device_id=where_is(peer), device_id_type=pl.DeviceIdType.MESH,
        )

    barrier = pltpu.get_barrier_semaphore()
    each(
        lambda peer: pl.semaphore_signal(
            barrier, inc=1, device_id=where_is(peer), device_id_type=pl.DeviceIdType.MESH
        )
    )

    loads = [
        pltpu.make_async_copy(source, target, load_sem.at[i])
        for i, (source, target) in enumerate(
            ((cid_hbm, cid_ref), (rank_hbm, rank_ref), (emb_hbm, emb_ref))
        )
    ]
    for load in loads:
        load.start()
    loads[0].wait()

    owner = cid_ref[...] % n
    before = (column(owner) == owner) & (iota((count, count), 0) < iota((count, count), 1))
    place = jnp.sum(before.astype(jnp.int32), axis=0, keepdims=True)
    owner_hot = iota((n, count), 0) == owner
    lane_hot = iota((LANES, count), 0) == place

    loads[1].wait()
    key = ((cid_ref[...] // n) * big + rank_ref[...] + 1).astype(jnp.float32)
    keys = dot(jnp.where(owner_hot, key, 0.0), lane_hot.astype(jnp.float32), NT, EXACT)
    lanes = iota((n, LANES), 1)
    missed = jnp.max(jnp.where(place >= sum(chunks), 1.0, 0.0), axis=1, keepdims=True)
    keys = jnp.where(lanes < sum(chunks), keys, jnp.where(lanes == LANES - 1, missed, 0.0))
    keys_out[...] = keys.reshape(n, 1, LANES)

    loads[2].wait()
    values = emb_ref[...].astype(jnp.float32)
    unit = (
        values * lax.rsqrt(jnp.sum(values * values, axis=1, keepdims=True) + epsilon)
    ).astype(jnp.bfloat16)

    def pack(piece, turn):
        size = chunks[piece]
        base = quarter_of(turn) * quarter
        local = place - starts[piece]
        slot = jnp.where((local >= 0) & (local < size), (owner - base) * size + local, -1)
        hot = (iota((quarter * size, count), 0) == slot).astype(jnp.bfloat16)
        packed = dot(hot, unit, NN).astype(jnp.bfloat16)
        rows_out[piece][pl.ds(base, quarter)] = packed.reshape(quarter, size, width)

    def send_keys(peer):
        return remote(
            keys_out.at[peer], keys_in.at[me], keys_out_sem, keys_in_sem, peer
        )

    others = pl.ds(0, n - 1)
    next_one = (me + 1) % n

    def take_keys():
        return remote(
            keys_out.at[others], keys_in.at[others], keys_out_sem, keys_in_sem, next_one
        )

    def send_rows(piece, peer):
        return remote(
            rows_out[piece].at[peer], rows_in[piece].at[me],
            rows_out_sem.at[piece], rows_in_sem.at[piece], peer,
        )

    def take_rows(piece):
        return remote(
            rows_out[piece].at[others], rows_in[piece].at[others],
            rows_out_sem.at[piece], rows_in_sem.at[piece], next_one,
        )

    def send_best(peer):
        return remote(
            best_out.at[peer], best_in.at[me], best_out_sem, best_in_sem, peer
        )

    def take_best():
        return remote(
            best_out.at[others], best_in.at[others], best_out_sem, best_in_sem, next_one
        )

    own = [
        pltpu.make_async_copy(rows_out[piece].at[me], rows_in[piece].at[me], own_sem.at[piece])
        for piece in range(pieces)
    ]
    own_keys = pltpu.make_async_copy(keys_out.at[me], keys_in.at[me], own_sem.at[pieces])
    own_best = pltpu.make_async_copy(best_out.at[me], best_in.at[me], own_sem.at[pieces + 1])

    for turn in range(4):
        pack(0, turn)
    pl.semaphore_wait(barrier, n - 1)
    for piece in range(pieces):
        for turn in range(4):
            if piece > 0:
                pack(piece, turn)
            each(lambda peer: send_rows(piece, peer).start(), (turn,))
        own[piece].start()
        if piece == 0:
            each(lambda peer: send_keys(peer).start())
            own_keys.start()

    take_keys().wait_recv()
    own_keys.wait()
    got = keys_in[...].reshape(n, LANES)
    over_ref[0, 0] = jnp.max(jnp.where(lanes == LANES - 1, got, 0.0))
    key_rows, key_columns, floors, spreads, sources = [], [], [], [], []
    for size, start in zip(chunks, starts):
        block = n * size
        source = (iota((n, block), 1) // size == iota((n, block), 0)).astype(jnp.float32)
        spread = iota((LANES, block), 0) == iota((LANES, block), 1) % size + start
        by_lane = dot(got, source, TN, EXACT)
        row = jnp.sum(jnp.where(spread, by_lane, 0.0), axis=0, keepdims=True)
        key_rows.append(row)
        key_columns.append(column(row))
        floors.append(jnp.floor(row * (1.0 / big)) * big)
        spreads.append(spread.astype(jnp.float32))
        sources.append(source)

    best = [jnp.full((1, n * size), -1.0, jnp.float32) for size in chunks]
    for piece, size in enumerate(chunks):
        take_rows(piece).wait_recv()
        own[piece].wait()
        here = rows_in[piece][...].reshape(n * size, width)
        for other in range(piece + 1):
            there = rows_in[other][...].reshape(n * chunks[other], width)
            pairs = [(here, piece, there, other)]
            if other != piece:
                pairs.append((there, other, here, piece))
            for members, m, queries, q in pairs:
                scores = dot(members, queries, NT)
                allowed = (key_columns[m] > floors[q]) & (key_columns[m] < key_rows[q])
                top = jnp.max(jnp.where(allowed, scores, -1.0), axis=0, keepdims=True)
                best[q] = jnp.maximum(best[q], top)
    answer = jnp.zeros((n, LANES), jnp.float32)
    for piece in range(pieces):
        answer = answer + dot(sources[piece] * best[piece], spreads[piece], NT, EXACT)
    best_out[...] = answer.reshape(n, 1, LANES)
    each(lambda peer: send_best(peer).start(), (2, 0, 1, 3))
    own_best.start()

    take_keys().wait_send()
    for piece in range(pieces):
        take_rows(piece).wait_send()
    take_best().wait_recv()
    own_best.wait()
    by_row = dot(best_in[...].reshape(n, LANES), owner_hot.astype(jnp.float32), TN, EXACT)
    out_ref[...] = jnp.sum(jnp.where(lane_hot, by_row, 0.0), axis=0, keepdims=True)
    take_best().wait_send()


def exchange(embeddings, cluster_ids, ranks, chunks, number):
    splits = lax.axis_size("split")
    n = lax.axis_size("loader") * splits
    count, width = embeddings.shape
    big = 1 << (n * count + 1).bit_length()
    dma = pltpu.SemaphoreType.DMA
    vmem = pl.BlockSpec(memory_space=pltpu.VMEM)
    rows = [pltpu.VMEM((n, size, width), jnp.bfloat16) for size in chunks]
    return pl.pallas_call(
        functools.partial(kernel, n, splits, chunks, big),
        out_shape=(
            jax.ShapeDtypeStruct((1, count), jnp.float32),
            jax.ShapeDtypeStruct((1, 1), jnp.float32),
        ),
        in_specs=[pl.BlockSpec(memory_space=pl.ANY)] * 3,
        out_specs=(vmem, pl.BlockSpec(memory_space=pltpu.SMEM)),
        scratch_shapes=[
            *rows,
            *rows,
            *[pltpu.VMEM((n, 1, LANES), jnp.float32)] * 4,
            dma((len(chunks),)),
            dma((len(chunks),)),
            *[dma] * 4,
            dma((len(chunks) + 2,)),
            pltpu.VMEM((count, width), embeddings.dtype),
            pltpu.VMEM((1, count), jnp.int32),
            pltpu.VMEM((1, count), jnp.int32),
            dma((3,)),
        ],
        compiler_params=pltpu.CompilerParams(collective_id=number, has_side_effects=True, vmem_limit_bytes=None if number == 0 else 67_043_328),
    )(embeddings, cluster_ids, ranks)


PLANES = 4
POOL = 20
STRIP = 4
EXTRA = 8


def pooled_kernel(
    n, splits, big, emb_hbm, cid_hbm, rank_hbm, out_ref, over_ref,
    emb_ref, cid_ref, rank_ref, rows_out, rows_in, pool_out, pool_in, extra_out, extra_in,
    meta_out, meta_in, keys_out, keys_in, best_out, best_in,
    load_sem, rows_out_sem, rows_in_sem, pool_sem, meta_sem, extra_sem, keys_sem, best_sem, ready,
):
    me = lax.axis_index("loader") * splits + lax.axis_index("split")
    count, width = emb_hbm.shape
    wide = n // PLANES
    z, j = me // wide, me % wide
    upper = z // 2
    farthest = 3 - 3 * upper
    order = (farthest, farthest - 1 + 2 * upper, 1 - z + 4 * upper, z)
    rows_of = wide // splits
    chip = j // 2

    def position(inner):
        return inner, inner // splits, inner % splits

    def near(turn, core):
        other = chip + turn
        return position(2 * jnp.where(other >= wide // 2, other - wide // 2, other) + core)

    partner = position(j + 1 - 2 * (j % 2))
    column_pair = (position(j), partner)
    around = [near(turn, core) for turn in range(1, wide // 2) for core in range(2)]

    def at(plane, spot):
        return plane * wide + spot[0], {"loader": plane * rows_of + spot[1], "split": spot[2]}

    def everyone(act):
        for peer in range(n):
            where = {"loader": peer // splits, "split": peer % splits}
            pl.when(me != peer)(functools.partial(act, peer, where))

    def remote(source, target, send, receive, peer):
        return pltpu.make_async_remote_copy(
            src_ref=source, dst_ref=target, send_sem=send, recv_sem=receive,
            device_id=peer, device_id_type=pl.DeviceIdType.MESH,
        )

    def signal(semaphore, peer):
        pl.semaphore_signal(semaphore, inc=1, device_id=peer, device_id_type=pl.DeviceIdType.MESH)

    barrier = pltpu.get_barrier_semaphore()
    for turn in range(3):
        for spot in column_pair:
            signal(barrier, at(order[turn], spot)[1])
    for spot in (partner, *around):
        signal(barrier, at(z, spot)[1])

    bands = 4
    band = count // bands
    pairs = [(cid_hbm, cid_ref), (rank_hbm, rank_ref)]
    for i in range(bands):
        rows = pl.ds(i * band, band)
        pairs.append((emb_hbm.at[rows], emb_ref.at[rows]))
    loads = [
        pltpu.make_async_copy(source, target, load_sem.at[i])
        for i, (source, target) in enumerate(pairs)
    ]
    for load in (loads[0], *loads[2:], loads[1]):
        load.start()
    earlier = (iota((count, count), 0) < iota((count, count), 1)).astype(jnp.bfloat16)
    loads[0].wait()

    owner = cid_ref[...] % n
    plane = owner // wide
    owner_hot = iota((n, count), 0) == owner
    so_far = dot(owner_hot.astype(jnp.bfloat16), earlier, NN)
    place = jnp.sum(jnp.where(owner_hot, so_far, 0.0), axis=0, keepdims=True).astype(jnp.int32)
    spill = jnp.maximum(so_far - TILE, 0.0)
    pooled = jnp.zeros((1, count), jnp.float32)
    for p in range(PLANES):
        here = jnp.sum(spill[p * wide : (p + 1) * wide], axis=0, keepdims=True)
        pooled = jnp.where(plane == p, here, pooled)
    pooled = pooled.astype(jnp.int32)
    spilled = place >= TILE
    fits = (place < TILE + EXTRA) & (pooled < POOL)
    turned = (z + 2 * PLANES - 1 - plane) % PLANES
    pool_row = jnp.where(spilled & fits, turned * POOL + pooled, -1)
    pool_hot = (iota((LANES, count), 0) == pool_row).astype(jnp.bfloat16)
    units = []
    for i in range(bands):
        loads[2 + i].wait()
        values = emb_ref[i * band : (i + 1) * band].astype(jnp.float32)
        scale = lax.rsqrt(jnp.sum(values * values, axis=1, keepdims=True) + epsilon)
        units.append((values * scale).astype(jnp.bfloat16))
    unit = jnp.concatenate(units, axis=0)
    strips = POOL // STRIP
    pool = dot(pool_hot[: PLANES * POOL], unit, NN).astype(jnp.bfloat16)
    pool_out[...] = pool.reshape(PLANES * strips, STRIP, width)
    own_pool = pl.ds((PLANES - 1) * strips, strips)
    pool_in[own_pool] = pool_out[own_pool]
    slot = jnp.where(spilled, -1, owner * TILE + place)

    def pack(plane):
        size = wide * TILE
        hot = (iota((size, count), 0) + plane * size == slot).astype(jnp.bfloat16)
        packed = dot(hot, unit, NN).astype(jnp.bfloat16)
        rows_out[pl.ds(plane * wide, wide)] = packed.reshape(wide, TILE, width)

    def send_rows(plane, spots):
        for spot in spots:
            peer, where = at(plane, spot)
            remote(
                rows_out.at[peer], rows_in.at[me], rows_out_sem, rows_in_sem.at[z], where
            ).start()

    others = pl.ds(0, n - 1)
    next_one = at(z, partner)[1]
    pools = pl.ds(0, (PLANES - 1) * strips)
    fellows = pl.ds(0, wide - 1)
    take_pools = remote(
        pool_out.at[pools], pool_in.at[pools], pool_sem.at[0], pool_sem.at[1], next_one
    )
    take_meta = remote(
        meta_in.at[pl.ds(0, PLANES - 1)], meta_in.at[pl.ds(0, PLANES - 1)],
        meta_sem.at[0], meta_sem.at[1], next_one,
    )
    take_extra = remote(
        extra_out.at[fellows], extra_in.at[fellows], extra_sem.at[0], extra_sem.at[1], next_one
    )
    take_keys = remote(
        keys_out.at[others], keys_in.at[others], keys_sem.at[0], keys_sem.at[1], next_one
    )
    take_best = remote(
        best_in.at[others], best_in.at[others], best_sem.at[0], best_sem.at[1], next_one
    )
    sent_rows = remote(
        rows_out.at[others], rows_in.at[others], rows_out_sem, rows_in_sem.at[0], next_one
    )

    def take_rows(source, many):
        block = pl.ds(0, many)
        remote(
            rows_out.at[block], rows_in.at[block], rows_out_sem, rows_in_sem.at[source], next_one
        ).wait_recv()

    def send_pool(plane):
        step = (z + 2 * PLANES - 1 - plane) % PLANES
        block = pl.ds(step * strips, strips)
        where = at(plane, column_pair[0])[1]
        remote(
            pool_out.at[block], pool_in.at[block], pool_sem.at[0], pool_sem.at[1], where
        ).start()

    def send_meta(plane):
        step = (z + 2 * PLANES - 1 - plane) % PLANES
        where = at(plane, column_pair[0])[1]
        remote(meta_out, meta_in.at[step], meta_sem.at[0], meta_sem.at[1], where).start()

    pl.semaphore_wait(barrier, 2 * (PLANES - 1) + wide - 1)
    for turn in range(3):
        send_pool(order[turn])
    for spot in around:
        signal(ready, at(z, spot)[1])
    code = ((owner % wide) * EXTRA + place - TILE + 1).astype(jnp.float32)
    code = jnp.broadcast_to(jnp.where(spilled, code, 0.0), (8, count)).astype(jnp.bfloat16)
    meta_out[...] = dot(code, pool_hot, NT)[:1]
    meta_in[PLANES - 1] = meta_out[...]
    for turn in range(3):
        send_meta(order[turn])
    for turn in range(3):
        pack(order[turn])
        send_rows(order[turn], column_pair)
    pack(z)
    rows_in[me] = rows_out[me]
    send_rows(z, [partner, *around])
    loads[1].wait()
    lanes = iota((n, LANES), 1)
    lane_hot = iota((LANES, count), 0) == place
    key = ((cid_ref[...] // n) * big + rank_ref[...] + 1).astype(jnp.float32)
    keys = dot(jnp.where(owner_hot, key, 0.0), lane_hot.astype(jnp.float32), NT, EXACT)
    missed = jnp.max(jnp.where(spilled & ~fits, 1.0, 0.0), axis=1, keepdims=True)
    keys = jnp.where(lanes < TILE + EXTRA, keys, jnp.where(lanes == LANES - 1, missed, 0.0))
    keys_out[...] = keys.reshape(n, 1, LANES)
    pl.semaphore_wait(ready, wide - 2)

    def send_keys(peer, where):
        remote(
            keys_out.at[peer], keys_in.at[me], keys_sem.at[0], keys_sem.at[1], where
        ).start()

    everyone(send_keys)
    keys_in[me] = keys_out[me]

    take_meta.wait_recv()
    segment = iota((1, LANES), 1) // POOL
    codes = jnp.full((1, LANES), -1.0, jnp.float32)
    for step in range(PLANES):
        got = meta_in[step]
        codes = jnp.where((segment == step) & (got > 0.0), got + step * 128.0, codes)
    codes = codes[:, : PLANES * POOL]
    block = wide * PLANES * EXTRA
    shape = (block, PLANES * POOL)
    line = iota(shape, 0)
    wanted = (line // EXTRA % PLANES) * 128 + line // (PLANES * EXTRA) * EXTRA + line % EXTRA + 1
    expand = (wanted.astype(jnp.float32) == codes).astype(jnp.bfloat16)
    take_pools.wait_recv()
    send_rows(order[0], around)
    expanded = dot(expand, pool_in[...].reshape(PLANES * POOL, width), NN).astype(jnp.bfloat16)
    extra_out[...] = expanded.reshape(wide, PLANES * EXTRA, width)
    extra_in[j] = extra_out[j]

    for spot in (partner, *around):
        remote(
            extra_out.at[spot[0]], extra_in.at[j], extra_sem.at[0], extra_sem.at[1],
            at(z, spot)[1],
        ).start()
    send_rows(order[1], around)
    send_rows(order[2], around)

    take_keys.wait_recv()
    over_ref[0, 0] = jnp.max(jnp.where(lanes == LANES - 1, keys_in[...].reshape(n, LANES), 0.0))
    row = iota((wide, LANES), 0)

    def keys_of(source):
        return keys_in[pl.ds(source * wide, wide)].reshape(wide, LANES)

    def plane_keys(source):
        spread = pltpu.roll(keys_of(source), 0, 1, stride=TILE, stride_axis=0)
        mine = iota((wide, LANES), 1) // TILE == row
        return jnp.sum(jnp.where(mine, spread, 0.0), axis=0, keepdims=True)

    run = PLANES * EXTRA
    per_tile = LANES // run
    lane = iota((wide, LANES), 1)
    run_keys = jnp.zeros((wide, LANES), jnp.float32)
    for step in range(PLANES):
        got = keys_of((z + 1 + step) % PLANES)
        moved = pltpu.roll(got, (step * EXTRA - TILE) % LANES, 1)
        run_keys = jnp.where(lane // EXTRA == step, moved, run_keys)
    repeated = run_keys
    for turn in range(1, per_tile):
        repeated = repeated + pltpu.roll(run_keys, turn * run, 1)
    repeated = jnp.where(lane // run == row % per_tile, repeated, 0.0)
    halves = [
        jnp.sum(repeated[first : first + per_tile], axis=0, keepdims=True)
        for first in range(0, wide, per_tile)
    ]

    def keyed(line):
        return line, column(line), jnp.floor(line * (1.0 / big)) * big

    sources = (order[3], None, order[2], order[0], order[1])
    keyring, best = [], []
    for source in sources:
        if source is None:
            line = jnp.concatenate(halves, axis=1)
        else:
            line = plane_keys(source)
        keyring.append(keyed(line))
        best.append(jnp.full(line.shape, -1.0, jnp.float32))

    def fetch(index):
        if sources[index] is None:
            return extra_in[...].reshape(block, width)
        return rows_in[pl.ds(sources[index] * wide, wide)].reshape(wide * TILE, width)

    def score(members, m, queries, q):
        scores = dot(members, queries, NT)
        key_row, _, floor = keyring[q]
        key_column = keyring[m][1]
        allowed = (key_column > floor) & (key_column < key_row)
        top = jnp.max(jnp.where(allowed, scores, -1.0), axis=0, keepdims=True)
        best[q] = jnp.maximum(best[q], top)

    def arrive(index):
        if sources[index] is None:
            take_extra.wait_recv()
        else:
            take_rows(sources[index], wide - 1 if index == 0 else wide)

    def answer(index):
        plane = sources[index]
        for half in range(tiles):
            best_out[plane * tiles + half, 0:1] = best[index]
            best_out[plane * tiles + half, 1:2] = best[1][:, half * LANES : (half + 1) * LANES]

        def send_best(inner):
            peer, where = at(plane, (inner, inner // splits, inner % splits))
            remote(
                best_out.at[plane * tiles + inner // per_tile], best_in.at[me],
                best_sem.at[0], best_sem.at[1], where,
            ).start()

        for inner in range(wide):
            if index == 0:
                pl.when(j != inner)(functools.partial(send_best, inner))
            else:
                send_best(inner)

    tiles = wide // per_tile
    last = len(sources) - 1
    for index in range(last):
        arrive(index)
        new = fetch(index)
        for other in range(index):
            old = fetch(other)
            if index < 3 or other > 0:
                score(new, index, old, other)
            score(old, other, new, index)
        score(new, index, new, index)
    arrive(last)
    new = fetch(last)
    for other in (1, 3, 2, 0):
        if other == 0:
            score(fetch(3), 3, fetch(0), 0)
        score(new, last, fetch(other), other)
        if other != 1:
            answer(other)
    for other in range(last):
        score(fetch(other), other, new, last)
    score(new, last, new, last)
    answer(last)
    best_in[me] = best_out[z * tiles + j // per_tile]

    take_pools.wait_send()
    for step in range(PLANES - 1):
        remote(meta_out, meta_in.at[step], meta_sem.at[0], meta_sem.at[1], next_one).wait_send()
    take_keys.wait_send()
    take_extra.wait_send()
    sent_rows.wait_send()
    take_best.wait_recv()
    answers = pltpu.roll(best_in[:, 0, :], (LANES - j * TILE) % LANES, 1)
    spare = best_in[:, 1, :]
    shifted = []
    for p in range(PLANES):
        step = (z + 2 * PLANES - 1 - p) % PLANES
        begin = j % per_tile * PLANES * EXTRA + step * EXTRA
        shifted.append(
            pltpu.roll(spare[p * wide : (p + 1) * wide], (LANES + TILE - begin) % LANES, 1)
        )
    table = jnp.where(lanes < TILE, answers, jnp.concatenate(shifted, axis=0))
    kept = 2 * TILE
    by_row = dot(table[:, :kept], owner_hot.astype(jnp.float32), TN, EXACT)
    out_ref[...] = jnp.sum(jnp.where(lane_hot[:kept], by_row, 0.0), axis=0, keepdims=True)
    take_best.wait_send()


def pooled_exchange(embeddings, cluster_ids, ranks):
    splits = lax.axis_size("split")
    n = lax.axis_size("loader") * splits
    count, width = embeddings.shape
    big = 1 << (n * count + 1).bit_length()
    wide = n // PLANES
    dma = pltpu.SemaphoreType.DMA

    def held(*shape):
        return pltpu.VMEM(shape, jnp.bfloat16)

    def told(*shape):
        return pltpu.VMEM(shape, jnp.float32)

    return pl.pallas_call(
        functools.partial(pooled_kernel, n, splits, big),
        out_shape=(
            jax.ShapeDtypeStruct((1, count), jnp.float32),
            jax.ShapeDtypeStruct((1, 1), jnp.float32),
        ),
        in_specs=[pl.BlockSpec(memory_space=pl.ANY)] * 3,
        out_specs=(
            pl.BlockSpec(memory_space=pltpu.VMEM), pl.BlockSpec(memory_space=pltpu.SMEM)
        ),
        scratch_shapes=[
            pltpu.VMEM((count, width), embeddings.dtype),
            pltpu.VMEM((1, count), jnp.int32),
            pltpu.VMEM((1, count), jnp.int32),
            *[held(n, TILE, width)] * 2,
            *[held(PLANES * POOL // STRIP, STRIP, width)] * 2,
            *[held(wide, PLANES * EXTRA, width)] * 2,
            told(1, LANES),
            told(PLANES, 1, LANES),
            *[told(n, 1, LANES)] * 2,
            told(PLANES * (wide * PLANES * EXTRA // LANES), 2, LANES),
            told(n, 2, LANES),
            dma((6,)),
            dma,
            dma((PLANES,)),
            *[dma((2,))] * 5,
            pltpu.SemaphoreType.REGULAR,
        ],
        compiler_params=pltpu.CompilerParams(collective_id=0, has_side_effects=True),
    )(embeddings, cluster_ids, ranks)


def two_sizes(embeddings, cluster_ids, ranks):
    n = lax.axis_size("loader") * lax.axis_size("split")
    count = embeddings.shape[0]
    cluster_ids, ranks = cluster_ids.reshape(1, count), ranks.reshape(1, count)
    most = CLUSTERS // n * CAP
    small, over = pooled_exchange(embeddings, cluster_ids, ranks)
    out = lax.cond(
        over[0, 0] > 0.0,
        lambda: exchange(embeddings, cluster_ids, ranks, (TILE, most - TILE), 1)[0],
        lambda: small,
    )
    return out.reshape(count)


def tile_scores(queries, remote):
    return jnp.einsum("kqd,kmd->kqm", queries, remote, preferred_element_type=jnp.float32)


def row_maxima(scores, query_rank, member_rank):
    allowed = (member_rank[:, None, :] >= 0) & (member_rank[:, None, :] < query_rank[:, :, None])
    return jnp.max(jnp.where(allowed, scores, jnp.float32(-1.0)), axis=2)


def small_tiles(embeddings, cluster_ids, ranks):
    loader_count = lax.axis_size("loader")
    split_count = lax.axis_size("split")
    rows_here = embeddings.shape[0]
    width = embeddings.shape[1]
    values = embeddings.astype(jnp.float32)
    unit = (values * lax.rsqrt(jnp.sum(values * values, axis=1, keepdims=True) + epsilon)).astype(
        jnp.bfloat16
    )
    cluster = cluster_ids[:, 0]
    row_index = jnp.arange(rows_here, dtype=jnp.int32)
    same_cluster = cluster[:, None] == cluster[None, :]
    earlier = row_index[None, :] < row_index[:, None]
    position = jnp.sum((same_cluster & earlier).astype(jnp.int32), axis=1)
    slot_count = CLUSTERS * CAP
    device_count = loader_count * split_count
    owner_flat = cluster % device_count
    cluster_slot = cluster // device_count
    owned = CLUSTERS // device_count
    target = (
        (cluster_slot * loader_count + owner_flat // split_count) * split_count
        + owner_flat % split_count
    ) * CAP + position
    send_rows = (
        jnp.zeros((slot_count, width), jnp.bfloat16)
        .at[target]
        .set(unit)
        .reshape(owned, loader_count, split_count, CAP, width)
    )
    send_rank = (
        jnp.full((slot_count,), -1, jnp.int32)
        .at[target]
        .set(ranks)
        .reshape(owned, loader_count, split_count, CAP)
    )

    def swap(block):
        return lax.all_to_all(
            lax.all_to_all(block, "loader", split_axis=1, concat_axis=1, tiled=True),
            "split",
            split_axis=2,
            concat_axis=2,
            tiled=True,
        )

    members = swap(send_rows).reshape(owned, -1, width)
    member_rank = swap(send_rank).reshape(owned, -1)
    best = row_maxima(tile_scores(members, members), member_rank, member_rank)
    returned = swap(best.reshape(owned, loader_count, split_count, CAP))
    return returned.reshape(-1)[target]


def shards(embeddings, cluster_ids, ranks):
    n = lax.axis_size("loader") * lax.axis_size("split")
    fits = n % 4 == 0 and CLUSTERS // n * CAP == 2 * TILE
    return (two_sizes if fits else small_tiles)(embeddings, cluster_ids, ranks)


def solution(mesh):
    return jax.shard_map(
        shards,
        mesh=mesh,
        in_specs=(
            P(("loader", "split"), None),
            P(("loader", "split"), None),
            P(("loader", "split")),
        ),
        out_specs=P(("loader", "split")),
        check_vma=False,
    )
```

profile of v0, /device:TPU:0, one launch (start us, length us, event | category | flops | bytes accessed | tf_op | source)
XLA Modules:
  0.0 34.0 jit_solution(14575042329388026190)
XLA Ops:
  0.0 32.8 %shard_map.39 = (f32[1,512]{1,0:T(1,128)S(1)}, f32[1,1]{1,0:T(1,128)}) custom-call(bf16[512,768]{1,0:T(8,128)(2,1)} %emb_hbm.1, s32[1,512]{1,0:T(1,128)} %bitcast.2.cid_hbm, s32[1,512]{1,0:T(1,128)} %bitcast.3.rank_hbm), custom_call_target="tpu_custom_call" | custom-call | tf_op jit(solution)/shard_map/pallas_call | solution.py:617
  33.4 0.6 %copy.10 = f32[512]{0:T(512)} copy(f32[512]{0:T(512)S(1)} %get-tuple-element.25) | data formatting | bytes 4096
  (1 shorter events, 0.0 us)
where the time goes:
time: 34.1 us; the launch traced here: 34 us
  Pallas kernels  32.8 us (96%)
  between operations  0.64 us (2%)
  local copies, waits for them, and re-layouts  0.58 us (2%)
    pallas_call x1, Pallas kernels, pooled_exchange(): pl.pallas_call(functools.partial(pooled_kernel, n, splits, big), out_shap...  32.8 us

commit v1 on v0

--- a/solution.py
+++ b/solution.py
@@ -285,6 +285,8 @@
     partner = position(j + 1 - 2 * (j % 2))
     column_pair = (position(j), partner)
     around = [near(turn, core) for turn in range(1, wide // 2) for core in range(2)]
+    chips = [jnp.where(chip <= k, k + 1, k) for k in reversed(range(wide // 2 - 1))]
+    ranked = [position(2 * other + core) for core in range(2) for other in chips]
 
     def at(plane, spot):
         return plane * wide + spot[0], {"loader": plane * rows_of + spot[1], "split": spot[2]}
@@ -469,7 +471,7 @@
             extra_out.at[spot[0]], extra_in.at[j], extra_sem.at[0], extra_sem.at[1],
             at(z, spot)[1],
         ).start()
-    send_rows(order[1], around)
+    send_rows(order[1], ranked)
     send_rows(order[2], around)
 
     take_keys.wait_recv()
@@ -577,12 +579,6 @@
     answer(last)
     best_in[me] = best_out[z * tiles + j // per_tile]
 
-    take_pools.wait_send()
-    for step in range(PLANES - 1):
-        remote(meta_out, meta_in.at[step], meta_sem.at[0], meta_sem.at[1], next_one).wait_send()
-    take_keys.wait_send()
-    take_extra.wait_send()
-    sent_rows.wait_send()
     take_best.wait_recv()
     answers = pltpu.roll(best_in[:, 0, :], (LANES - j * TILE) % LANES, 1)
     spare = best_in[:, 1, :]
@@ -597,6 +593,12 @@
     kept = 2 * TILE
     by_row = dot(table[:, :kept], owner_hot.astype(jnp.float32), TN, EXACT)
     out_ref[...] = jnp.sum(jnp.where(lane_hot[:kept], by_row, 0.0), axis=0, keepdims=True)
+    take_pools.wait_send()
+    for step in range(PLANES - 1):
+        remote(meta_out, meta_in.at[step], meta_sem.at[0], meta_sem.at[1], next_one).wait_send()
+    take_keys.wait_send()
+    take_extra.wait_send()
+    sent_rows.wait_send()
     take_best.wait_send()
 
 
@@ -724,6 +726,7 @@
 def shards(embeddings, cluster_ids, ranks):
     n = lax.axis_size("loader") * lax.axis_size("split")
     fits = n % 4 == 0 and CLUSTERS // n * CAP == 2 * TILE
+    fits = fits and n // PLANES % lax.axis_size("split") == 0
     return (two_sizes if fits else small_tiles)(embeddings, cluster_ids, ranks)
 
 

time: 34.1 us -> 33.3 us (0.977)
  Pallas kernels: 32.8 us -> 32 us
    pallas_call x1, Pallas kernels: 32.8 us -> 32 us  [pooled_exchange(): pl.pallas_call(functools.partial(pooled_kernel, n, splits, big), out_shap...]
where the time goes in v1:
time: 33.3 us; the launch traced here: 33.2 us
  Pallas kernels  32 us (96%)
  between operations  0.64 us (2%)
  local copies, waits for them, and re-layouts  0.58 us (2%)
    pallas_call x1, Pallas kernels, pooled_exchange(): pl.pallas_call(functools.partial(pooled_kernel, n, splits, big), out_shap...  32 us

profile of v1, /device:TPU:0, one launch (start us, length us, event | category | flops | bytes accessed | tf_op | source)
XLA Modules:
  0.0 33.2 jit_solution(16788182332595114564)
XLA Ops:
  0.0 32.0 %shard_map.39 = (f32[1,512]{1,0:T(1,128)S(1)}, f32[1,1]{1,0:T(1,128)}) custom-call(bf16[512,768]{1,0:T(8,128)(2,1)} %emb_hbm.1, s32[1,512]{1,0:T(1,128)} %bitcast.2.cid_hbm, s32[1,512]{1,0:T(1,128)} %bitcast.3.rank_hbm), custom_call_target="tpu_custom_call" | custom-call | tf_op jit(solution)/shard_map/pallas_call | solution.py:619
  32.6 0.6 %copy.10 = f32[512]{0:T(512)} copy(f32[512]{0:T(512)S(1)} %get-tuple-element.25) | data formatting | bytes 4096
  (1 shorter events, 0.0 us)

commit v2 on v1

--- a/solution.py
+++ b/solution.py
@@ -462,6 +462,7 @@
     expand = (wanted.astype(jnp.float32) == codes).astype(jnp.bfloat16)
     take_pools.wait_recv()
     send_rows(order[0], around)
+    send_rows(order[1], ranked[:5])
     expanded = dot(expand, pool_in[...].reshape(PLANES * POOL, width), NN).astype(jnp.bfloat16)
     extra_out[...] = expanded.reshape(wide, PLANES * EXTRA, width)
     extra_in[j] = extra_out[j]
@@ -471,8 +472,8 @@
             extra_out.at[spot[0]], extra_in.at[j], extra_sem.at[0], extra_sem.at[1],
             at(z, spot)[1],
         ).start()
-    send_rows(order[1], ranked)
     send_rows(order[2], around)
+    send_rows(order[1], ranked[5:])
 
     take_keys.wait_recv()
     over_ref[0, 0] = jnp.max(jnp.where(lanes == LANES - 1, keys_in[...].reshape(n, LANES), 0.0))

time: 33.3 us -> 33.3 us (level)
  no operation moved by 1% of the time
where the time goes in v2:
time: 33.3 us; the launch traced here: 33.2 us
  Pallas kernels  32 us (96%)
  between operations  0.64 us (2%)
  local copies, waits for them, and re-layouts  0.58 us (2%)
    pallas_call x1, Pallas kernels, pooled_exchange(): pl.pallas_call(functools.partial(pooled_kernel, n, splits, big), out_shap...  32 us

profile of v2, /device:TPU:0, one launch (start us, length us, event | category | flops | bytes accessed | tf_op | source)
XLA Modules:
  0.0 33.2 jit_solution(3666970193317697952)
XLA Ops:
  0.0 32.0 %shard_map.39 = (f32[1,512]{1,0:T(1,128)S(1)}, f32[1,1]{1,0:T(1,128)}) custom-call(bf16[512,768]{1,0:T(8,128)(2,1)} %emb_hbm.1, s32[1,512]{1,0:T(1,128)} %bitcast.2.cid_hbm, s32[1,512]{1,0:T(1,128)} %bitcast.3.rank_hbm), custom_call_target="tpu_custom_call" | custom-call | tf_op jit(solution)/shard_map/pallas_call | solution.py:620
  32.6 0.6 %copy.10 = f32[512]{0:T(512)} copy(f32[512]{0:T(512)S(1)} %get-tuple-element.25) | data formatting | bytes 4096
  (1 shorter events, 0.0 us)
